TPU v7x, 512 devices: a whole 4x8x8 slice. The times are simulated.
512 devices in a mesh: dp: 256 (over x, y, z), outer: 2 (over core).
Axes of the slice: x: 4, y: 8, z: 8, core: 2. Of those that a mesh axis runs over, the one named last changes fastest.
Arguments:
- gradient: float32 [512, 131072], P(('dp', 'outer')), may hold values from -6 to 6
- residual: float32 [512, 131072], P(('dp', 'outer')), may hold values from -6 to 6
- indices: int32 [512, 512], P(('dp', 'outer')), may hold values from 0 to 131071, as said below
- params: float32 [131072], replicated, may hold values from -6 to 6
Outputs:
- new_params: float32 [131072], replicated
- new_residual: float32 [512, 131072], P(('dp', 'outer'))
Inputs may be any that keep to these rules, and one draw needn't show every extreme that they name: Within each worker's row the 512 indices are distinct and increasing: index j lies in [j * 256, (j + 1) * 256). Different workers often pick the same coordinate.
All inputs are finite; a program needn't handle non-finite values.
Results may differ from a plain program's by a relative error of at most 0.0003.
Values sent between devices are 32-bit elements.
No kernel may reach another device: no remote copies, remote signals or barrier semaphores. Data moves between devices by JAX's collectives and lax.ppermute only.
A program may use at most 64 MiB of HBM per device.

v0:
```python
import jax
import jax.numpy as jnp
from jax import lax
from jax.sharding import Mesh
from jax.sharding import PartitionSpec as P

DP_OUTER = ("dp_0", "dp_1", "dp_2", "outer")


step_size = 0.5


def split_up(array, dim, devices):
    return jnp.stack(jnp.split(array, devices, axis=dim))


def scatter_pairs(array, chips, core, dim):
    sizes = lax.axis_size(chips), lax.axis_size(core)
    parts = split_up(array, dim, sizes[0] * sizes[1])
    inside = parts.shape[1:]
    parts = parts.reshape(*sizes, *inside).swapaxes(0, 1).reshape(-1, *inside)
    parts = lax.psum_scatter(parts, core, scatter_dimension=0, tiled=True)
    return lax.psum_scatter(parts, chips, scatter_dimension=0, tiled=True)[0]


def shards(gradient, residual, indices, params):
    accumulated = gradient[0] + residual[0]
    positions = indices[0]
    values_sent = accumulated[positions]
    new_residual = accumulated.at[positions].set(jnp.float32(0.0))[None, :]
    empty = jnp.zeros((accumulated.shape[0],), jnp.float32)
    spread = empty.at[positions].add(values_sent)
    portion = scatter_pairs(spread, ("dp_0", "dp_1", "dp_2"), "outer", 0)
    length = portion.shape[0]
    first = lax.axis_index(DP_OUTER) * length
    own_params = lax.dynamic_slice_in_dim(params, first, length)
    updated = own_params - step_size * portion
    new_params = lax.all_gather(updated, DP_OUTER, axis=0, tiled=True)
    return (new_params, new_residual)


def solution(mesh):
    torus = Mesh(
        mesh.devices.reshape(4, 8, 8, mesh.shape["outer"]), ("dp_0", "dp_1", "dp_2", "outer")
    )
    placed = (P(DP_OUTER, None), P(DP_OUTER, None), P(DP_OUTER, None), P())
    return jax.shard_map(
        shards, mesh=torus, in_specs=placed, out_specs=(P(), P(DP_OUTER, None)), check_vma=False
    )
```

profile of v0, /device:TPU:1, one launch (start us, length us, event | category | flops | bytes accessed | tf_op | source)
XLA Modules:
  0.0 373.6 jit_solution(5409333906929286416)
XLA Ops:
  7.2 0.0 reduce-scatter.2.cloned.1.call-start
  7.2 0.7 compare_select_fusion
  7.9 1.7 add.41
  9.7 3.1 gather_fusion
  12.8 3.7 scatter_custom_fusion
  17.0 0.8 concatenate
  17.9 0.8 concatenate.1
  18.7 0.3 reshape.41
  19.0 0.8 copy.7
  19.9 0.0 reduce-scatter.2.cloned.1.call-update
  19.9 0.0 all-reduce.3.cloned.1.call-start
  19.9 23.1 %reduce-scatter.2.cloned.1.call-done = f32[256,256]{1,0:T(8,128)} async-done(((f32[512,256]{1,0:T(8,128)}), f32[256,256]{1,0:T(8,128)}) %reduce-scatter.2.cloned.1.call-update) | async-done | bytes 262160 | tf_op jit(solution)/shard_map/reduce_scatter | solution.py:22
  43.0 0.0 all-reduce.3.cloned.1.call-update
  43.1 2.7 scatter_fusion
  45.8 0.0 copy-start
  45.8 1.3 dynamic-slice
  47.1 238.9 %all-reduce.3.cloned.1.call-done = f32[256,256]{1,0:T(8,128)} async-done(((f32[256,256]{1,0:T(8,128)}), f32[256,256]{1,0:T(8,128)}) %all-reduce.3.cloned.1.call-update) | async-done | bytes 262160
  286.0 1.3 dynamic-slice_multiply_fusion
  287.4 0.8 dynamic-slice_subtract_fusion
  288.1 77.8 %all-gather = f32[512,1,256]{2,1,0:T(1,128)S(1)} all-gather(f32[1,1,256]{2,1,0:T(1,128)S(1)} %bitcast.1044), channel_id=1, replica_groups=mesh['dp_0'=4,'dp_1'=8,'dp_2'=8,'outer'=2] {'dp_0','dp_1','dp_2','outer'}, dimensions={0}, use_global_device_ids=true | all-gather | bytes 525312 | tf_op jit(solution)/shard_map/all_gather | solution.py:38
  366.0 0.8 copy.11
  366.8 0.0 copy-done
  (31 shorter events, 0.4 us)
Async XLA Ops:
  7.2 35.9 %reduce-scatter.2.cloned.1.call-start = ((), (), s32[]{:S(2)}) async-start(), calls=%async_computation.1 | async-start | bytes 786432 | tf_op jit(solution)/shard_map/reduce_scatter | solution.py:22
  19.9 266.1 %all-reduce.3.cloned.1.call-start = ((), (), s32[]{:S(2)}) async-start(), calls=%async_computation.2 | async-start | bytes 524288
  45.8 321.0 %copy-start = (f32[131072]{0:T(1024)}, f32[131072]{0:T(1024)S(1)}, u32[]{:S(2)}) copy-start(f32[131072]{0:T(1024)S(1)} %scatter_fusion) | copy-start | bytes 1572868
Sparse Core Ops, SparseCore 0:
  20.0 22.9 reduce-scatter.1
  48.0 238.0 all-reduce.2
where the time goes:
time: 374 us
  waiting for transfers between devices  262 us (70%)
  blocking collectives  77.8 us (21%)
  between operations  14.3 us (4%)
  local copies, waits for them, and re-layouts  11.1 us (3%)
  other arithmetic  8.24 us (2%)
    unnamed x3, waiting for transfers between devices  239 us
    all_gather x1, blocking collectives, shards(): new_params = lax.all_gather(updated, DP_OUTER, axis=0, tiled=True)  77.8 us
    reduce_scatter x1, waiting for transfers between devices, scatter_pairs(): parts = lax.psum_scatter(parts, core, scatter_dimension=0, tiled=True)  23.1 us
  transfers between devices with their start and end apart: 2, of which 2 were waited for; matrix products, arithmetic and copies ran while one was open for 1% of the time, Pallas kernels for 0%

commit v1 on v0

v1 whole, which is shorter than its diff:
```python
import jax
import jax.numpy as jnp
from jax import lax
from jax.experimental import pallas as pl
from jax.experimental.pallas import tpu as pltpu
from jax.sharding import Mesh
from jax.sharding import PartitionSpec as P

AXES = ("x1", "x0", "y2", "y1", "y0", "z2", "z1", "z0", "outer")
NEAR = ("x1", "x0")
FAR = tuple(a for a in AXES if a not in NEAR and a != "outer")
NS = 2 ** len(NEAR)
NT = 2 ** len(FAR)
NB = 256 // NS
PACK = 64 // NB
STEP = 0.5


def lanes(shape):
    return lax.broadcasted_iota(jnp.int32, shape, 1)


def pick_kernel(idx_ref, g_ref, r_ref, send_ref, res_ref, v_scr, o_scr):
    step = pl.program_id(0)
    off = (idx_ref[pl.ds(step, 1), :] & 255).astype(jnp.float32)
    col = jnp.transpose(jnp.broadcast_to(off, (128, 128)))
    lane = lanes((128, 128)).astype(jnp.float32)
    low = col == lane
    high = col == lane + 128.0
    even = pl.ds(0, 128, stride=2)
    odd = pl.ds(1, 128, stride=2)
    a0 = g_ref[even, :] + r_ref[even, :]
    a1 = g_ref[odd, :] + r_ref[odd, :]
    res_ref[even, :] = jnp.where(low, 0.0, a0)
    res_ref[odd, :] = jnp.where(high, 0.0, a1)
    hit = jnp.where(low, a0, jnp.where(high, a1, 0.0))
    v_scr[pl.ds(step, 1), :] = jnp.sum(jnp.transpose(hit), axis=0, keepdims=True)
    o_scr[pl.ds(step, 1), :] = off

    @pl.when(step == 3)
    def _():
        lane1 = lanes((1, 128))
        for s in range(NS):
            for c in range(2):
                block = c * 256 + s * NB
                row, at = block // 128, block % 128
                val = v_scr[row : row + 1, :]
                offs = o_scr[row : row + 1, :]
                left = pltpu.roll(val, (128 - at) % 128, 1) if at else val
                move = (NB - at) % 128
                right = pltpu.roll(offs, move, 1) if move else offs
                send_ref[s * 2 + c] = jnp.where(lane1 < NB, left, right)[:, : 2 * NB]


def pick(idx, g, r):
    return pl.pallas_call(
        pick_kernel,
        grid=(4,),
        in_specs=[
            pl.BlockSpec((4, 128), lambda i: (0, 0)),
            pl.BlockSpec((256, 128), lambda i: (i, 0)),
            pl.BlockSpec((256, 128), lambda i: (i, 0)),
        ],
        out_specs=[
            pl.BlockSpec((2 * NS, 1, 2 * NB), lambda i: (0, 0, 0)),
            pl.BlockSpec((256, 128), lambda i: (i, 0)),
        ],
        out_shape=[
            jax.ShapeDtypeStruct((2 * NS, 1, 2 * NB), jnp.float32),
            jax.ShapeDtypeStruct((1024, 128), jnp.float32),
        ],
        scratch_shapes=[pltpu.VMEM((4, 128), jnp.float32), pltpu.VMEM((4, 128), jnp.float32)],
        name="pick",
    )(idx, g, r)


def copies_kernel(in_ref, out_ref, scr):
    for p in range(8):
        rows = [in_ref[p + 8 * i] for i in range(PACK)]
        scr[p : p + 1, :] = rows[0] if PACK == 1 else jnp.concatenate(rows, axis=1)
    whole = scr[...]
    for t in range(NT):
        out_ref[t] = whole


def copies(pairs):
    return pl.pallas_call(
        copies_kernel,
        out_shape=jax.ShapeDtypeStruct((NT, 8, 128), jnp.float32),
        scratch_shapes=[pltpu.VMEM((8, 128), jnp.float32)],
        name="copies",
    )(pairs)


GROUP = 8


def total_kernel(where_ref, w_ref, p_ref, out_ref, tot):
    lane = lanes((8, 128)).astype(jnp.float32)
    lane_high = lane + 128.0
    for k0 in range(0, NB, GROUP):

        def body(t, accs):
            w = w_ref[t]
            accs = list(accs)
            for i in range(PACK):
                for k in range(GROUP):
                    at = i * 2 * NB + k0 + k
                    val = jnp.broadcast_to(w[:, at : at + 1], (8, 128))
                    off = jnp.broadcast_to(w[:, at + NB : at + NB + 1], (8, 128))
                    accs[2 * k] += jnp.where(off == lane, val, 0.0)
                    accs[2 * k + 1] += jnp.where(off == lane_high, val, 0.0)
            return tuple(accs)

        accs = lax.fori_loop(0, NT, body, (jnp.zeros((8, 128), jnp.float32),) * (2 * GROUP))
        for n, acc in enumerate(accs):
            tot[2 * k0 + n : 2 * k0 + n + 1, :] = jnp.sum(acc, axis=0, keepdims=True)
    new = p_ref[...] - STEP * tot[...]
    for s in range(NS):
        out_ref[s] = new


def total(where, pairs, params):
    rows = 2 * NB
    return pl.pallas_call(
        total_kernel,
        grid_spec=pltpu.PrefetchScalarGridSpec(
            num_scalar_prefetch=1,
            grid=(1,),
            in_specs=[
                pl.BlockSpec((NT, 8, 128), lambda i, at: (0, 0, 0)),
                pl.BlockSpec((rows, 128), lambda i, at: (at[0], 0)),
            ],
            out_specs=pl.BlockSpec((NS, rows, 128), lambda i, at: (0, 0, 0)),
            scratch_shapes=[pltpu.VMEM((rows, 128), jnp.float32)],
        ),
        out_shape=jax.ShapeDtypeStruct((NS, rows, 128), jnp.float32),
        name="total",
    )(where, pairs, params)


def shards(gradient, residual, indices, params):
    g = gradient.reshape(1024, 128)
    r = residual.reshape(1024, 128)
    idx = indices.reshape(4, 128)
    send, res = pick(idx, g, r)
    got = lax.all_to_all(send, NEAR + ("outer",), 0, 0)
    everyone = lax.all_to_all(copies(got), FAR, 0, 0)
    where = lax.axis_index("outer") * NS + lax.axis_index(NEAR)
    new = total(where.reshape(1).astype(jnp.int32), everyone, params.reshape(1024, 128))
    half = lax.all_to_all(new, NEAR, 0, 0)
    both = lax.all_gather(half.reshape(512, 128), "outer", axis=0, tiled=True)
    return both.reshape(131072), res.reshape(1, 131072)


def solution(mesh):
    torus = Mesh(mesh.devices.reshape((2,) * 9), AXES)
    placed = (P(AXES, None), P(AXES, None), P(AXES, None), P())
    return jax.shard_map(
        shards, mesh=torus, in_specs=placed, out_specs=(P(), P(AXES, None)), check_vma=False
    )
```

time: 374 us -> 113 us (0.30)
  waiting for transfers between devices: 262 us -> 12.8 us
  Pallas kernels: 0 us -> 55.7 us
  blocking collectives: 77.8 us -> 30.2 us
  between operations: 14.3 us -> 0.65 us
  starting transfers between devices: 0.08 us -> 11.5 us
  local copies, waits for them, and re-layouts: 11.1 us -> 1.53 us
  other arithmetic: 8.24 us -> 0 us
    unnamed x3 -> x0, waiting for transfers between devices: 239 us -> none
    all_gather x1, blocking collectives: 77.8 us -> 6.22 us  [shards(): both = lax.all_gather(half.reshape(512, 128), 'outer', axis=0, tiled=True)]
    pallas_call x0 -> x3, Pallas kernels: none -> 55.7 us  [the longest x1 50.5 us: total(): pl.pallas_call(total_kernel, grid_spec=pltpu.PrefetchScalarGridSpec(num_s...]
    all_to_all x0 -> x2, blocking collectives: none -> 24 us  [the longest x1 15.1 us: shards(): got = lax.all_to_all(send, NEAR + ('outer',), 0, 0)]
    reduce_scatter x1 -> x0, waiting for transfers between devices: 23.1 us -> none  [scatter_pairs(): parts = lax.psum_scatter(parts, core, scatter_dimension=0, tiled=True)]
    all_to_all x0 -> x1, waiting for transfers between devices: none -> 12.8 us  [shards(): everyone = lax.all_to_all(copies(got), FAR, 0, 0)]
    all_to_all x0 -> x1, starting transfers between devices: none -> 11.5 us  [shards(): everyone = lax.all_to_all(copies(got), FAR, 0, 0)]
  transfers between devices with their start and end apart: 2 -> 1, of which waited for: 2 -> 1; matrix products, arithmetic and copies ran while one was open for 1% -> 0% of each run, Pallas kernels for 0% -> 0%
where the time goes in v1:
time: 113 us; the launch traced here: 112 us
  Pallas kernels  55.7 us (49%)
  blocking collectives  30.2 us (27%)
  waiting for transfers between devices  12.8 us (11%)
  starting transfers between devices  11.5 us (10%)
  local copies, waits for them, and re-layouts  1.53 us (1%)
    pallas_call x1, Pallas kernels, total(): pl.pallas_call(total_kernel, grid_spec=pltpu.PrefetchScalarGridSpec(num_s...  50.5 us
    all_to_all x1, blocking collectives, shards(): got = lax.all_to_all(send, NEAR + ('outer',), 0, 0)  15.1 us
    all_to_all x1, waiting for transfers between devices, shards(): everyone = lax.all_to_all(copies(got), FAR, 0, 0)  12.8 us
    all_to_all x1, starting transfers between devices, shards(): everyone = lax.all_to_all(copies(got), FAR, 0, 0)  11.5 us
    all_to_all x1, blocking collectives, shards(): half = lax.all_to_all(new, NEAR, 0, 0)  8.9 us
    all_gather x1, blocking collectives, shards(): both = lax.all_gather(half.reshape(512, 128), 'outer', axis=0, tiled=True)  6.22 us
    pallas_call x1, Pallas kernels, pick(): pl.pallas_call(pick_kernel, grid=(4,), in_specs=[pl.BlockSpec((4, 128), l...  3.73 us
  transfers between devices with their start and end apart: 1, of which 1 were waited for; matrix products, arithmetic and copies ran while one was open for 0% of the time, Pallas kernels for 0%

profile of v1, /device:TPU:1, one launch (start us, length us, event | category | flops | bytes accessed | tf_op | source)
XLA Modules:
  0.0 112.4 jit_solution(3774819716859489305)
XLA Ops:
  0.6 3.7 %pick.1 = (f32[8,1,128]{2,1,0:T(1,128)}, f32[1024,128]{1,0:T(8,128)}) custom-call(s32[4,128]{1,0:T(4,128)} %bitcast.13, f32[1024,128]{1,0:T(8,128)} %bitcast.10, f32[1024,128]{1,0:T(8,128)} %bitcast.11), custom_call_target="tpu_custom_call" | custom-call | tf_op jit(solution)/shard_map/pick/pallas_call | solution.py:56
  4.4 15.1 %all_to_all.15.in_ref = f32[8,1,128]{2,1,0:T(1,128)} all-to-all(f32[8,1,128]{2,1,0:T(1,128)} %get-tuple-element.4), channel_id=1, replica_groups=mesh['x1'=2,'x0'=2,'y2'=2,'y1'=2,'y0'=2,'z2'=2,'z1'=2,'z0'=2,'outer'=2] ..., dimensions={0} | all-to-all | bytes 8192 | tf_op jit(solution)/shard_map/all_to_all | solution.py:147
  19.4 1.4 %copies.1 = f32[64,8,128]{2,1,0:T(8,128)} custom-call(f32[8,1,128]{2,1,0:T(1,128)} %all_to_all.15.in_ref), custom_call_target="tpu_custom_call" | custom-call | tf_op jit(solution)/shard_map/copies/pallas_call | solution.py:87
  20.8 11.5 %all-to-all-start.1 = ((f32[64,8,128]{2,1,0:T(8,128)}), f32[64,8,128]{2,1,0:T(8,128)S(1)}, u32[]{:S(2)}, u32[]{:S(2)}) async-start(f32[64,8,128]{2,1,0:T(8,128)} %copies.1), calls=%async_computation.1 | async-start | bytes 524288 | tf_op jit(solution)/shard_map/all_to_all | solution.py:148
  32.4 12.8 %all-to-all-done.1.w_ref = f32[64,8,128]{2,1,0:T(8,128)S(1)} async-done(((f32[64,8,128]{2,1,0:T(8,128)}), f32[64,8,128]{2,1,0:T(8,128)S(1)}, u32[]{:S(2)}, u32[]{:S(2)}) %all-to-all-start.1) | async-done | bytes 262176 | tf_op jit(solution)/shard_map/all_to_all | solution.py:148
  45.2 0.0 copy-start
  45.2 0.7 copy-done
  45.9 50.5 %total.1 = f32[4,128,128]{2,1,0:T(8,128)} custom-call(s32[1]{0:T(128)} %bitcast.where_ref, f32[64,8,128]{2,1,0:T(8,128)} %copy-done, f32[1024,128]{1,0:T(8,128)} %bitcast.12), custom_call_target="tpu_custom_call" | custom-call | tf_op jit(solution)/shard_map/total/pallas_call | solution.py:125
  96.4 8.9 %all_to_all.16 = f32[4,128,128]{2,1,0:T(8,128)S(1)} all-to-all(f32[4,128,128]{2,1,0:T(8,128)} %total.1), channel_id=1, replica_groups=mesh['x1'=2,'x0'=2,'y2'=2,'y1'=2,'y0'=2,'z2'=2,'z1'=2,'z0'=2,'outer'=2] ..., dimensions={0} | all-to-all | bytes 524288 | tf_op jit(solution)/shard_map/all_to_all | solution.py:151
  105.4 6.2 %all_gather.3 = f32[1024,128]{1,0:T(8,128)S(1)} all-gather(f32[512,128]{1,0:T(8,128)S(1)} %bitcast.9), channel_id=1, replica_groups=mesh['x1'=2,'x0'=2,'y2'=2,'y1'=2,'y0'=2,'z2'=2,'z1'=2,'z0'=2,'outer'=2] ..., dimensions={0}, use_global_device_ids=true | all-gather | bytes 786432 | tf_op jit(solution)/shard_map/all_gather | solution.py:152
  111.6 0.8 copy.7
Async XLA Ops:
  20.8 24.4 %all-to-all-start.1 = ((f32[64,8,128]{2,1,0:T(8,128)}), f32[64,8,128]{2,1,0:T(8,128)S(1)}, u32[]{:S(2)}, u32[]{:S(2)}) async-start(f32[64,8,128]{2,1,0:T(8,128)} %copies.1), calls=%async_computation.1 | async-start | bytes 524288 | tf_op jit(solution)/shard_map/all_to_all | solution.py:148
  45.2 0.7 copy-start

commit v2 on v1

--- a/solution.py
+++ b/solution.py
@@ -66,7 +66,7 @@
             pl.BlockSpec((256, 128), lambda i: (i, 0)),
         ],
         out_shape=[
-            jax.ShapeDtypeStruct((2 * NS, 1, 2 * NB), jnp.float32),
+            pltpu.VMEM((2 * NS, 1, 2 * NB), jnp.float32),
             jax.ShapeDtypeStruct((1024, 128), jnp.float32),
         ],
         scratch_shapes=[pltpu.VMEM((4, 128), jnp.float32), pltpu.VMEM((4, 128), jnp.float32)],
@@ -83,38 +83,64 @@
         out_ref[t] = whole
 
 
+def near(x):
+    return pltpu.with_memory_space_constraint(x, pltpu.VMEM)
+
+
 def copies(pairs):
     return pl.pallas_call(
         copies_kernel,
-        out_shape=jax.ShapeDtypeStruct((NT, 8, 128), jnp.float32),
+        out_shape=pltpu.VMEM((NT, 8, 128), jnp.float32),
         scratch_shapes=[pltpu.VMEM((8, 128), jnp.float32)],
         name="copies",
-    )(pairs)
+    )(near(pairs))
 
 
 GROUP = 8
+ROWS = 512 // PACK
 
 
-def total_kernel(where_ref, w_ref, p_ref, out_ref, tot):
-    lane = lanes((8, 128)).astype(jnp.float32)
-    lane_high = lane + 128.0
+def total_kernel(where_ref, w_ref, p_ref, out_ref, turned, tot):
+    whole = w_ref[...].reshape(ROWS, 128)
+    for n in range(ROWS // 128):
+        turned[:, 128 * n : 128 * n + 128] = jnp.transpose(whole[128 * n : 128 * n + 128, :])
+    digit = lax.broadcasted_iota(jnp.int32, (16, ROWS), 0).astype(jnp.float32)
+    row = lax.broadcasted_iota(jnp.int32, (128, 128), 0)
+    lane = lanes((128, 128))
+    own = (row // 16) == (lane // 16)
+    spot = (row % 8) == (lane // 16)
     for k0 in range(0, NB, GROUP):
-
-        def body(t, accs):
-            w = w_ref[t]
-            accs = list(accs)
-            for i in range(PACK):
-                for k in range(GROUP):
-                    at = i * 2 * NB + k0 + k
-                    val = jnp.broadcast_to(w[:, at : at + 1], (8, 128))
-                    off = jnp.broadcast_to(w[:, at + NB : at + NB + 1], (8, 128))
-                    accs[2 * k] += jnp.where(off == lane, val, 0.0)
-                    accs[2 * k + 1] += jnp.where(off == lane_high, val, 0.0)
-            return tuple(accs)
-
-        accs = lax.fori_loop(0, NT, body, (jnp.zeros((8, 128), jnp.float32),) * (2 * GROUP))
-        for n, acc in enumerate(accs):
-            tot[2 * k0 + n : 2 * k0 + n + 1, :] = jnp.sum(acc, axis=0, keepdims=True)
+        acc = jnp.zeros((128, 128), jnp.float32)
+        for i in range(PACK):
+            parts = ([], [], [])
+            right = []
+            at = i * 2 * NB + k0
+            val = turned[at : at + GROUP, :]
+            off = turned[at + NB : at + NB + GROUP, :]
+            first = val.astype(jnp.bfloat16).astype(jnp.float32)
+            rest = val - first
+            second = rest.astype(jnp.bfloat16).astype(jnp.float32)
+            third = rest - second
+            hi = jnp.floor(off * 0.0625)
+            lo = off - 16.0 * hi
+            for k in range(GROUP):
+                hot = digit == hi[k : k + 1, :]
+                for m, part in enumerate((first, second, third)):
+                    parts[m].append(jnp.where(hot, part[k : k + 1, :], 0.0).astype(jnp.bfloat16))
+                right.append(jnp.where(digit == lo[k : k + 1, :], 1.0, 0.0).astype(jnp.bfloat16))
+            right = jnp.concatenate(right, axis=0)
+            for m in range(3):
+                acc += lax.dot_general(
+                    jnp.concatenate(parts[m], axis=0),
+                    right,
+                    (((1,), (1,)), ((), ())),
+                    preferred_element_type=jnp.float32,
+                )
+        acc = jnp.where(own, acc, 0.0)
+        for turn in (64, 32, 16):
+            acc = acc + pltpu.roll(acc, turn, 1)
+        acc = jnp.where(spot, acc, 0.0)
+        tot[2 * k0 : 2 * k0 + 16, :] = jnp.sum(acc.reshape(16, 8, 128), axis=1)
     new = p_ref[...] - STEP * tot[...]
     for s in range(NS):
         out_ref[s] = new
@@ -132,22 +158,23 @@
                 pl.BlockSpec((rows, 128), lambda i, at: (at[0], 0)),
             ],
             out_specs=pl.BlockSpec((NS, rows, 128), lambda i, at: (0, 0, 0)),
-            scratch_shapes=[pltpu.VMEM((rows, 128), jnp.float32)],
+            scratch_shapes=[pltpu.VMEM((128, ROWS), jnp.float32), pltpu.VMEM((rows, 128), jnp.float32)],
         ),
-        out_shape=jax.ShapeDtypeStruct((NS, rows, 128), jnp.float32),
+        out_shape=pltpu.VMEM((NS, rows, 128), jnp.float32),
         name="total",
-    )(where, pairs, params)
+    )(where, near(pairs), params)
 
 
 def shards(gradient, residual, indices, params):
     g = gradient.reshape(1024, 128)
     r = residual.reshape(1024, 128)
     idx = indices.reshape(4, 128)
+    where = (lax.axis_index("outer") * NS + lax.axis_index(NEAR)).reshape(1).astype(jnp.int32)
+    where, idx = lax.optimization_barrier((where, idx))
     send, res = pick(idx, g, r)
     got = lax.all_to_all(send, NEAR + ("outer",), 0, 0)
     everyone = lax.all_to_all(copies(got), FAR, 0, 0)
-    where = lax.axis_index("outer") * NS + lax.axis_index(NEAR)
-    new = total(where.reshape(1).astype(jnp.int32), everyone, params.reshape(1024, 128))
+    new = total(where, everyone, params.reshape(1024, 128))
     half = lax.all_to_all(new, NEAR, 0, 0)
     both = lax.all_gather(half.reshape(512, 128), "outer", axis=0, tiled=True)
     return both.reshape(131072), res.reshape(1, 131072)

time: 113 us -> 61.1 us (0.54)
  Pallas kernels: 55.7 us -> 6.02 us
  blocking collectives: 30.2 us -> 53.3 us
  waiting for transfers between devices: 12.8 us -> 0 us
  starting transfers between devices: 11.5 us -> 0 us
    pallas_call x1, Pallas kernels: 50.5 us -> 2.27 us  [total(): pl.pallas_call(total_kernel, grid_spec=pltpu.PrefetchScalarGridSpec(num_s...]
    all_to_all x0 -> x1, blocking collectives: none -> 25.7 us  [shards(): everyone = lax.all_to_all(copies(got), FAR, 0, 0)]
    all_to_all x1 -> x0, waiting for transfers between devices: 12.8 us -> none  [shards(): everyone = lax.all_to_all(copies(got), FAR, 0, 0)]
    all_to_all x1 -> x0, starting transfers between devices: 11.5 us -> none  [shards(): everyone = lax.all_to_all(copies(got), FAR, 0, 0)]
    pallas_call x1, Pallas kernels: 1.4 us -> 0.02 us  [copies(): pl.pallas_call(copies_kernel, out_shape=pltpu.VMEM((NT, 8, 128), jnp.floa...]
    all_to_all x1, blocking collectives: 15.1 us -> 13.8 us  [shards(): got = lax.all_to_all(send, NEAR + ('outer',), 0, 0)]
  transfers between devices with their start and end apart: 1 -> 0, of which waited for: 1 -> 0; matrix products, arithmetic and copies ran while one was open for 0% -> 0% of each run, Pallas kernels for 0% -> 0%
where the time goes in v2:
time: 61.1 us; the launch traced here: 60.8 us
  blocking collectives  53.3 us (87%)
  Pallas kernels  6.02 us (10%)
  local copies, waits for them, and re-layouts  0.83 us (1%)
  between operations  0.65 us (1%)
    all_to_all x1, blocking collectives, shards(): everyone = lax.all_to_all(copies(got), FAR, 0, 0)  25.7 us
    all_to_all x1, blocking collectives, shards(): got = lax.all_to_all(send, NEAR + ('outer',), 0, 0)  13.8 us
    all_to_all x1, blocking collectives, shards(): half = lax.all_to_all(new, NEAR, 0, 0)  7.92 us
    all_gather x1, blocking collectives, shards(): both = lax.all_gather(half.reshape(512, 128), 'outer', axis=0, tiled=True)  5.92 us
    pallas_call x1, Pallas kernels, pick(): pl.pallas_call(pick_kernel, grid=(4,), in_specs=[pl.BlockSpec((4, 128), l...  3.73 us
    pallas_call x1, Pallas kernels, total(): pl.pallas_call(total_kernel, grid_spec=pltpu.PrefetchScalarGridSpec(num_s...  2.27 us

profile of v2, /device:TPU:1, one launch (start us, length us, event | category | flops | bytes accessed | tf_op | source)
XLA Modules:
  0.0 60.8 jit_solution(7142817154144562732)
XLA Ops:
  0.6 3.7 %pick.1 = (f32[8,1,128]{2,1,0:T(1,128)S(1)}, f32[1024,128]{1,0:T(8,128)}) custom-call(s32[4,128]{1,0:T(4,128)} %bitcast.13, f32[1024,128]{1,0:T(8,128)} %bitcast.10, f32[1024,128]{1,0:T(8,128)} %bitcast.11), custom_call_target="tpu_custom_call" | custom-call | tf_op jit(solution)/shard_map/pick/pallas_call | solution.py:56
  4.4 13.8 %all_to_all.15.in_ref = f32[8,1,128]{2,1,0:T(1,128)S(1)} all-to-all(f32[8,1,128]{2,1,0:T(1,128)S(1)} %get-tuple-element.8), channel_id=1, replica_groups=mesh['x1'=2,'x0'=2,'y2'=2,'y1'=2,'y0'=2,'z2'=2,'z1'=2,'z0'=2,'outer'=2] ..., dimensions={0} | all-to-all | bytes 8192 | tf_op jit(solution)/shard_map/all_to_all | solution.py:175
  18.2 25.7 %all_to_all.16.w_ref = f32[64,8,128]{2,1,0:T(8,128)S(1)} all-to-all(f32[64,8,128]{2,1,0:T(8,128)S(1)} %copies.1), channel_id=1, replica_groups=mesh['x1'=2,'x0'=2,'y2'=2,'y1'=2,'y0'=2,'z2'=2,'z1'=2,'z0'=2,'outer'=2] ..., dimensions={0} | all-to-all | bytes 524288 | tf_op jit(solution)/shard_map/all_to_all | solution.py:176
  43.9 2.3 %total.1 = f32[4,128,128]{2,1,0:T(8,128)S(1)} custom-call(s32[1]{0:T(128)} %bitcast.where_ref, f32[64,8,128]{2,1,0:T(8,128)S(1)} %all_to_all.16.w_ref, f32[1024,128]{1,0:T(8,128)} %bitcast.12), custom_call_target="tpu_custom_call" | custom-call | tf_op jit(solution)/shard_map/total/pallas_call | solution.py:151
  46.2 7.9 %all_to_all.17 = f32[4,128,128]{2,1,0:T(8,128)S(1)} all-to-all(f32[4,128,128]{2,1,0:T(8,128)S(1)} %total.1), channel_id=1, replica_groups=mesh['x1'=2,'x0'=2,'y2'=2,'y1'=2,'y0'=2,'z2'=2,'z1'=2,'z0'=2,'outer'=2] ..., dimensions={0} | all-to-all | bytes 524288 | tf_op jit(solution)/shard_map/all_to_all | solution.py:178
  54.1 5.9 %all_gather.3 = f32[1024,128]{1,0:T(8,128)S(1)} all-gather(f32[512,128]{1,0:T(8,128)S(1)} %bitcast.9), channel_id=1, replica_groups=mesh['x1'=2,'x0'=2,'y2'=2,'y1'=2,'y0'=2,'z2'=2,'z1'=2,'z0'=2,'outer'=2] ..., dimensions={0}, use_global_device_ids=true | all-gather | bytes 786432 | tf_op jit(solution)/shard_map/all_gather | solution.py:179
  60.0 0.8 %copy.7 = f32[131072]{0:T(1024)} copy(f32[131072]{0:T(1024)S(1)} %bitcast.8) | data formatting | bytes 1048576
  (1 shorter events, 0.0 us)

commit v3 on v2

--- a/solution.py
+++ b/solution.py
@@ -20,56 +20,77 @@
     return lax.broadcasted_iota(jnp.int32, shape, 1)
 
 
-def pick_kernel(idx_ref, g_ref, r_ref, send_ref, res_ref, v_scr, o_scr):
-    step = pl.program_id(0)
-    off = (idx_ref[pl.ds(step, 1), :] & 255).astype(jnp.float32)
-    col = jnp.transpose(jnp.broadcast_to(off, (128, 128)))
+def pick_kernel(idx_ref, g_hbm, r_hbm, send_ref, res_hbm, g_ref, r_ref, res_ref, v_scr, o_scr, col_scr, g_sem, r_sem, res_sem):
+    def span(n):
+        return pl.ds(256 * n, 256)
+
+    loads = []
+    for n in range(4):
+        one = pltpu.make_async_copy(g_hbm.at[span(n)], g_ref.at[span(n)], g_sem.at[n])
+        two = pltpu.make_async_copy(r_hbm.at[span(n)], r_ref.at[span(n)], r_sem.at[n])
+        one.start()
+        two.start()
+        loads.append((one, two))
+    for n in range(4):
+        off = (idx_ref[n : n + 1, :] & 255).astype(jnp.float32)
+        o_scr[n : n + 1, :] = off
+        col_scr[n] = jnp.transpose(jnp.broadcast_to(off, (128, 128)))
     lane = lanes((128, 128)).astype(jnp.float32)
-    low = col == lane
-    high = col == lane + 128.0
-    even = pl.ds(0, 128, stride=2)
-    odd = pl.ds(1, 128, stride=2)
-    a0 = g_ref[even, :] + r_ref[even, :]
-    a1 = g_ref[odd, :] + r_ref[odd, :]
-    res_ref[even, :] = jnp.where(low, 0.0, a0)
-    res_ref[odd, :] = jnp.where(high, 0.0, a1)
-    hit = jnp.where(low, a0, jnp.where(high, a1, 0.0))
-    v_scr[pl.ds(step, 1), :] = jnp.sum(jnp.transpose(hit), axis=0, keepdims=True)
-    o_scr[pl.ds(step, 1), :] = off
-
-    @pl.when(step == 3)
-    def _():
-        lane1 = lanes((1, 128))
-        for s in range(NS):
-            for c in range(2):
-                block = c * 256 + s * NB
-                row, at = block // 128, block % 128
-                val = v_scr[row : row + 1, :]
-                offs = o_scr[row : row + 1, :]
-                left = pltpu.roll(val, (128 - at) % 128, 1) if at else val
-                move = (NB - at) % 128
-                right = pltpu.roll(offs, move, 1) if move else offs
-                send_ref[s * 2 + c] = jnp.where(lane1 < NB, left, right)[:, : 2 * NB]
+    stores = []
+    for n in range(4):
+        for load in loads[n]:
+            load.wait()
+        col = col_scr[n]
+        low = col == lane
+        high = col == lane + 128.0
+        even = pl.ds(256 * n, 128, stride=2)
+        odd = pl.ds(256 * n + 1, 128, stride=2)
+        a0 = g_ref[even, :] + r_ref[even, :]
+        a1 = g_ref[odd, :] + r_ref[odd, :]
+        res_ref[even, :] = jnp.where(low, 0.0, a0)
+        res_ref[odd, :] = jnp.where(high, 0.0, a1)
+        store = pltpu.make_async_copy(res_ref.at[span(n)], res_hbm.at[span(n)], res_sem.at[n])
+        store.start()
+        stores.append(store)
+        hit = jnp.where(low, a0, jnp.where(high, a1, 0.0))
+        v_scr[n : n + 1, :] = jnp.sum(jnp.transpose(hit), axis=0, keepdims=True)
+    lane1 = lanes((1, 128))
+    for s in range(NS):
+        for c in range(2):
+            block = c * 256 + s * NB
+            row, at = block // 128, block % 128
+            val = v_scr[row : row + 1, :]
+            offs = o_scr[row : row + 1, :]
+            left = pltpu.roll(val, (128 - at) % 128, 1) if at else val
+            move = (NB - at) % 128
+            right = pltpu.roll(offs, move, 1) if move else offs
+            send_ref[s * 2 + c] = jnp.where(lane1 < NB, left, right)[:, : 2 * NB]
+    for store in stores:
+        store.wait()
 
 
 def pick(idx, g, r):
+    in_hbm = pl.BlockSpec(memory_space=pltpu.HBM)
+    in_vmem = pl.BlockSpec(memory_space=pltpu.VMEM)
     return pl.pallas_call(
         pick_kernel,
-        grid=(4,),
-        in_specs=[
-            pl.BlockSpec((4, 128), lambda i: (0, 0)),
-            pl.BlockSpec((256, 128), lambda i: (i, 0)),
-            pl.BlockSpec((256, 128), lambda i: (i, 0)),
-        ],
-        out_specs=[
-            pl.BlockSpec((2 * NS, 1, 2 * NB), lambda i: (0, 0, 0)),
-            pl.BlockSpec((256, 128), lambda i: (i, 0)),
-        ],
+        in_specs=[in_vmem, in_hbm, in_hbm],
+        out_specs=[in_vmem, in_hbm],
         out_shape=[
             pltpu.VMEM((2 * NS, 1, 2 * NB), jnp.float32),
             jax.ShapeDtypeStruct((1024, 128), jnp.float32),
         ],
-        scratch_shapes=[pltpu.VMEM((4, 128), jnp.float32), pltpu.VMEM((4, 128), jnp.float32)],
+        scratch_shapes=[
+            pltpu.VMEM((1024, 128), jnp.float32),
+            pltpu.VMEM((1024, 128), jnp.float32),
+            pltpu.VMEM((1024, 128), jnp.float32),
+            pltpu.VMEM((4, 128), jnp.float32),
+            pltpu.VMEM((4, 128), jnp.float32),
+            pltpu.VMEM((4, 128, 128), jnp.float32),
+            pltpu.SemaphoreType.DMA((4,)),
+            pltpu.SemaphoreType.DMA((4,)),
+            pltpu.SemaphoreType.DMA((4,)),
+        ],
         name="pick",
     )(idx, g, r)
 

time: 61.1 us -> 60.2 us (0.985)
  Pallas kernels: 6.02 us -> 5.08 us
    pallas_call x1, Pallas kernels: 3.73 us -> 2.79 us  [pick(): pl.pallas_call(pick_kernel, in_specs=[in_vmem, in_hbm, in_hbm], out_specs...]
where the time goes in v3:
time: 60.2 us; the launch traced here: 59.9 us
  blocking collectives  53.3 us (89%)
  Pallas kernels  5.08 us (8%)
  local copies, waits for them, and re-layouts  0.83 us (1%)
  between operations  0.66 us (1%)
    all_to_all x1, blocking collectives, shards(): everyone = lax.all_to_all(copies(got), FAR, 0, 0)  25.7 us
    all_to_all x1, blocking collectives, shards(): got = lax.all_to_all(send, NEAR + ('outer',), 0, 0)  13.8 us
    all_to_all x1, blocking collectives, shards(): half = lax.all_to_all(new, NEAR, 0, 0)  7.92 us
    all_gather x1, blocking collectives, shards(): both = lax.all_gather(half.reshape(512, 128), 'outer', axis=0, tiled=True)  5.92 us
    pallas_call x1, Pallas kernels, pick(): pl.pallas_call(pick_kernel, in_specs=[in_vmem, in_hbm, in_hbm], out_specs...  2.79 us
    pallas_call x1, Pallas kernels, total(): pl.pallas_call(total_kernel, grid_spec=pltpu.PrefetchScalarGridSpec(num_s...  2.27 us

profile of v3, /device:TPU:1, one launch (start us, length us, event | category | flops | bytes accessed | tf_op | source)
XLA Modules:
  0.0 59.9 jit_solution(12767085387210182910)
XLA Ops:
  0.6 2.8 %pick.1 = (f32[8,1,128]{2,1,0:T(1,128)S(1)}, f32[1024,128]{1,0:T(8,128)}) custom-call(s32[4,128]{1,0:T(4,128)} %bitcast.13, f32[1024,128]{1,0:T(8,128)} %bitcast.10, f32[1024,128]{1,0:T(8,128)} %bitcast.11), custom_call_target="tpu_custom_call" | custom-call | tf_op jit(solution)/shard_map/pick/pallas_call | solution.py:75
  3.4 13.8 %all_to_all.15.in_ref = f32[8,1,128]{2,1,0:T(1,128)S(1)} all-to-all(f32[8,1,128]{2,1,0:T(1,128)S(1)} %get-tuple-element.8), channel_id=1, replica_groups=mesh['x1'=2,'x0'=2,'y2'=2,'y1'=2,'y0'=2,'z2'=2,'z1'=2,'z0'=2,'outer'=2] ..., dimensions={0} | all-to-all | bytes 8192 | tf_op jit(solution)/shard_map/all_to_all | solution.py:196
  17.3 25.7 %all_to_all.16.w_ref = f32[64,8,128]{2,1,0:T(8,128)S(1)} all-to-all(f32[64,8,128]{2,1,0:T(8,128)S(1)} %copies.1), channel_id=1, replica_groups=mesh['x1'=2,'x0'=2,'y2'=2,'y1'=2,'y0'=2,'z2'=2,'z1'=2,'z0'=2,'outer'=2] ..., dimensions={0} | all-to-all | bytes 524288 | tf_op jit(solution)/shard_map/all_to_all | solution.py:197
  43.0 2.3 %total.1 = f32[4,128,128]{2,1,0:T(8,128)S(1)} custom-call(s32[1]{0:T(128)} %bitcast.where_ref, f32[64,8,128]{2,1,0:T(8,128)S(1)} %all_to_all.16.w_ref, f32[1024,128]{1,0:T(8,128)} %bitcast.12), custom_call_target="tpu_custom_call" | custom-call | tf_op jit(solution)/shard_map/total/pallas_call | solution.py:172
  45.2 7.9 %all_to_all.17 = f32[4,128,128]{2,1,0:T(8,128)S(1)} all-to-all(f32[4,128,128]{2,1,0:T(8,128)S(1)} %total.1), channel_id=1, replica_groups=mesh['x1'=2,'x0'=2,'y2'=2,'y1'=2,'y0'=2,'z2'=2,'z1'=2,'z0'=2,'outer'=2] ..., dimensions={0} | all-to-all | bytes 524288 | tf_op jit(solution)/shard_map/all_to_all | solution.py:199
  53.2 5.9 %all_gather.3 = f32[1024,128]{1,0:T(8,128)S(1)} all-gather(f32[512,128]{1,0:T(8,128)S(1)} %bitcast.9), channel_id=1, replica_groups=mesh['x1'=2,'x0'=2,'y2'=2,'y1'=2,'y0'=2,'z2'=2,'z1'=2,'z0'=2,'outer'=2] ..., dimensions={0}, use_global_device_ids=true | all-gather | bytes 786432 | tf_op jit(solution)/shard_map/all_gather | solution.py:200
  59.1 0.8 %copy.7 = f32[131072]{0:T(1024)} copy(f32[131072]{0:T(1024)S(1)} %bitcast.8) | data formatting | bytes 1048576
  (1 shorter events, 0.0 us)

commit v4 on v3

--- a/solution.py
+++ b/solution.py
@@ -7,7 +7,7 @@
 from jax.sharding import PartitionSpec as P
 
 AXES = ("x1", "x0", "y2", "y1", "y0", "z2", "z1", "z0", "outer")
-NEAR = ("x1", "x0")
+NEAR = ("x1", "x0", "y0")
 FAR = tuple(a for a in AXES if a not in NEAR and a != "outer")
 NS = 2 ** len(NEAR)
 NT = 2 ** len(FAR)

time: 60.2 us -> 58.4 us (0.970)
  blocking collectives: 53.3 us -> 52.1 us
    all_to_all x1, blocking collectives: 25.7 us -> 23.9 us  [shards(): everyone = lax.all_to_all(copies(got), FAR, 0, 0)]
    all_gather x1, blocking collectives: 5.92 us -> 4.84 us  [shards(): both = lax.all_gather(half.reshape(512, 128), 'outer', axis=0, tiled=True)]
    all_to_all x1, blocking collectives: 13.8 us -> 14.8 us  [shards(): got = lax.all_to_all(send, NEAR + ('outer',), 0, 0)]
    all_to_all x1, blocking collectives: 7.92 us -> 8.55 us  [shards(): half = lax.all_to_all(new, NEAR, 0, 0)]
where the time goes in v4:
time: 58.4 us; the launch traced here: 58.1 us
  blocking collectives  52.1 us (89%)
  Pallas kernels  4.55 us (8%)
  local copies, waits for them, and re-layouts  0.83 us (1%)
  between operations  0.66 us (1%)
    all_to_all x1, blocking collectives, shards(): everyone = lax.all_to_all(copies(got), FAR, 0, 0)  23.9 us
    all_to_all x1, blocking collectives, shards(): got = lax.all_to_all(send, NEAR + ('outer',), 0, 0)  14.8 us
    all_to_all x1, blocking collectives, shards(): half = lax.all_to_all(new, NEAR, 0, 0)  8.55 us
    all_gather x1, blocking collectives, shards(): both = lax.all_gather(half.reshape(512, 128), 'outer', axis=0, tiled=True)  4.84 us
    pallas_call x1, Pallas kernels, pick(): pl.pallas_call(pick_kernel, in_specs=[in_vmem, in_hbm, in_hbm], out_specs...  2.79 us
    pallas_call x1, Pallas kernels, total(): pl.pallas_call(total_kernel, grid_spec=pltpu.PrefetchScalarGridSpec(num_s...  1.67 us

profile of v4, /device:TPU:1, one launch (start us, length us, event | category | flops | bytes accessed | tf_op | source)
XLA Modules:
  0.0 58.1 jit_solution(10758880881561823940)
XLA Ops:
  0.6 2.8 %pick.1 = (f32[16,1,64]{2,1,0:T(1,128)S(1)}, f32[1024,128]{1,0:T(8,128)}) custom-call(s32[4,128]{1,0:T(4,128)} %bitcast.13, f32[1024,128]{1,0:T(8,128)} %bitcast.10, f32[1024,128]{1,0:T(8,128)} %bitcast.11), custom_call_target="tpu_custom_call" | custom-call | tf_op jit(solution)/shard_map/pick/pallas_call | solution.py:75
  3.4 14.8 %all_to_all.15.in_ref = f32[16,1,64]{2,1,0:T(1,128)S(1)} all-to-all(f32[16,1,64]{2,1,0:T(1,128)S(1)} %get-tuple-element.8), channel_id=1, replica_groups=mesh['x1'=2,'x0'=2,'y2'=2,'y1'=2,'y0'=2,'z2'=2,'z1'=2,'z0'=2,'outer'=2] ..., dimensions={0} | all-to-all | bytes 8192 | tf_op jit(solution)/shard_map/all_to_all | solution.py:196
  18.3 0.1 copies.1
  18.3 23.9 %all_to_all.16.w_ref = f32[32,8,128]{2,1,0:T(8,128)S(1)} all-to-all(f32[32,8,128]{2,1,0:T(8,128)S(1)} %copies.1), channel_id=1, replica_groups=mesh['x1'=2,'x0'=2,'y2'=2,'y1'=2,'y0'=2,'z2'=2,'z1'=2,'z0'=2,'outer'=2] ..., dimensions={0} | all-to-all | bytes 262144 | tf_op jit(solution)/shard_map/all_to_all | solution.py:197
  42.2 1.7 %total.1 = f32[8,64,128]{2,1,0:T(8,128)S(1)} custom-call(s32[1]{0:T(128)} %bitcast.where_ref, f32[32,8,128]{2,1,0:T(8,128)S(1)} %all_to_all.16.w_ref, f32[1024,128]{1,0:T(8,128)} %bitcast.12), custom_call_target="tpu_custom_call" | custom-call | tf_op jit(solution)/shard_map/total/pallas_call | solution.py:172
  43.9 8.5 %all_to_all.17 = f32[8,64,128]{2,1,0:T(8,128)S(1)} all-to-all(f32[8,64,128]{2,1,0:T(8,128)S(1)} %total.1), channel_id=1, replica_groups=mesh['x1'=2,'x0'=2,'y2'=2,'y1'=2,'y0'=2,'z2'=2,'z1'=2,'z0'=2,'outer'=2] ..., dimensions={0} | all-to-all | bytes 524288 | tf_op jit(solution)/shard_map/all_to_all | solution.py:199
  52.4 4.8 %all_gather.3 = f32[1024,128]{1,0:T(8,128)S(1)} all-gather(f32[512,128]{1,0:T(8,128)S(1)} %bitcast.9), channel_id=1, replica_groups=mesh['x1'=2,'x0'=2,'y2'=2,'y1'=2,'y0'=2,'z2'=2,'z1'=2,'z0'=2,'outer'=2] ..., dimensions={0}, use_global_device_ids=true | all-gather | bytes 786432 | tf_op jit(solution)/shard_map/all_gather | solution.py:200
  57.3 0.8 %copy.7 = f32[131072]{0:T(1024)} copy(f32[131072]{0:T(1024)S(1)} %bitcast.8) | data formatting | bytes 1048576

commit v5 on v4

--- a/solution.py
+++ b/solution.py
@@ -163,7 +163,7 @@
         acc = jnp.where(spot, acc, 0.0)
         tot[2 * k0 : 2 * k0 + 16, :] = jnp.sum(acc.reshape(16, 8, 128), axis=1)
     new = p_ref[...] - STEP * tot[...]
-    for s in range(NS):
+    for s in range(2 * NS):
         out_ref[s] = new
 
 
@@ -178,10 +178,10 @@
                 pl.BlockSpec((NT, 8, 128), lambda i, at: (0, 0, 0)),
                 pl.BlockSpec((rows, 128), lambda i, at: (at[0], 0)),
             ],
-            out_specs=pl.BlockSpec((NS, rows, 128), lambda i, at: (0, 0, 0)),
+            out_specs=pl.BlockSpec((2 * NS, rows, 128), lambda i, at: (0, 0, 0)),
             scratch_shapes=[pltpu.VMEM((128, ROWS), jnp.float32), pltpu.VMEM((rows, 128), jnp.float32)],
         ),
-        out_shape=pltpu.VMEM((NS, rows, 128), jnp.float32),
+        out_shape=pltpu.VMEM((2 * NS, rows, 128), jnp.float32),
         name="total",
     )(where, near(pairs), params)
 
@@ -196,8 +196,7 @@
     got = lax.all_to_all(send, NEAR + ("outer",), 0, 0)
     everyone = lax.all_to_all(copies(got), FAR, 0, 0)
     new = total(where, everyone, params.reshape(1024, 128))
-    half = lax.all_to_all(new, NEAR, 0, 0)
-    both = lax.all_gather(half.reshape(512, 128), "outer", axis=0, tiled=True)
+    both = lax.all_to_all(new, ("outer",) + NEAR, 0, 0)
     return both.reshape(131072), res.reshape(1, 131072)
 
 

time: 58.4 us -> 58.2 us (level)
    all_gather x1 -> x0, blocking collectives: 4.84 us -> none  [shards(): both = lax.all_gather(half.reshape(512, 128), 'outer', axis=0, tiled=True)]
    all_to_all x1, blocking collectives: 8.55 us -> 12.9 us  [shards(): both = lax.all_to_all(new, ('outer',) + NEAR, 0, 0)]
where the time goes in v5:
time: 58.2 us; the launch traced here: 57.6 us
  blocking collectives  51.6 us (89%)
  Pallas kernels  4.56 us (8%)
  local copies, waits for them, and re-layouts  0.83 us (1%)
  between operations  0.66 us (1%)
    all_to_all x1, blocking collectives, shards(): everyone = lax.all_to_all(copies(got), FAR, 0, 0)  23.9 us
    all_to_all x1, blocking collectives, shards(): got = lax.all_to_all(send, NEAR + ('outer',), 0, 0)  14.8 us
    all_to_all x1, blocking collectives, shards(): both = lax.all_to_all(new, ('outer',) + NEAR, 0, 0)  12.9 us
    pallas_call x1, Pallas kernels, pick(): pl.pallas_call(pick_kernel, in_specs=[in_vmem, in_hbm, in_hbm], out_specs...  2.79 us
    pallas_call x1, Pallas kernels, total(): pl.pallas_call(total_kernel, grid_spec=pltpu.PrefetchScalarGridSpec(num_s...  1.68 us

profile of v5, /device:TPU:1, one launch (start us, length us, event | category | flops | bytes accessed | tf_op | source)
XLA Modules:
  0.0 57.6 jit_solution(16533808652773228355)
XLA Ops:
  0.6 2.8 %pick.1 = (f32[16,1,64]{2,1,0:T(1,128)S(1)}, f32[1024,128]{1,0:T(8,128)}) custom-call(s32[4,128]{1,0:T(4,128)} %bitcast.11, f32[1024,128]{1,0:T(8,128)} %bitcast.8, f32[1024,128]{1,0:T(8,128)} %bitcast.9), custom_call_target="tpu_custom_call" | custom-call | tf_op jit(solution)/shard_map/pick/pallas_call | solution.py:75
  3.4 14.8 %all_to_all.15.in_ref = f32[16,1,64]{2,1,0:T(1,128)S(1)} all-to-all(f32[16,1,64]{2,1,0:T(1,128)S(1)} %get-tuple-element.8), channel_id=1, replica_groups=mesh['x1'=2,'x0'=2,'y2'=2,'y1'=2,'y0'=2,'z2'=2,'z1'=2,'z0'=2,'outer'=2] ..., dimensions={0} | all-to-all | bytes 8192 | tf_op jit(solution)/shard_map/all_to_all | solution.py:196
  18.3 0.1 copies.1
  18.3 23.9 %all_to_all.16.w_ref = f32[32,8,128]{2,1,0:T(8,128)S(1)} all-to-all(f32[32,8,128]{2,1,0:T(8,128)S(1)} %copies.1), channel_id=1, replica_groups=mesh['x1'=2,'x0'=2,'y2'=2,'y1'=2,'y0'=2,'z2'=2,'z1'=2,'z0'=2,'outer'=2] ..., dimensions={0} | all-to-all | bytes 262144 | tf_op jit(solution)/shard_map/all_to_all | solution.py:197
  42.2 1.7 %total.1 = f32[16,64,128]{2,1,0:T(8,128)S(1)} custom-call(s32[1]{0:T(128)} %bitcast.where_ref, f32[32,8,128]{2,1,0:T(8,128)S(1)} %all_to_all.16.w_ref, f32[1024,128]{1,0:T(8,128)} %bitcast.10), custom_call_target="tpu_custom_call" | custom-call | tf_op jit(solution)/shard_map/total/pallas_call | solution.py:172
  43.9 12.9 %all_to_all.17 = f32[16,64,128]{2,1,0:T(8,128)S(1)} all-to-all(f32[16,64,128]{2,1,0:T(8,128)S(1)} %total.1), channel_id=1, replica_groups=mesh['x1'=2,'x0'=2,'y2'=2,'y1'=2,'y0'=2,'z2'=2,'z1'=2,'z0'=2,'outer'=2] ..., dimensions={0} | all-to-all | bytes 1048576 | tf_op jit(solution)/shard_map/all_to_all | solution.py:199
  56.8 0.8 %copy.7 = f32[131072]{0:T(1024)} copy(f32[131072]{0:T(1024)S(1)} %bitcast.7) | data formatting | bytes 1048576

commit v6 on v5

--- a/solution.py
+++ b/solution.py
@@ -64,7 +64,7 @@
             left = pltpu.roll(val, (128 - at) % 128, 1) if at else val
             move = (NB - at) % 128
             right = pltpu.roll(offs, move, 1) if move else offs
-            send_ref[s * 2 + c] = jnp.where(lane1 < NB, left, right)[:, : 2 * NB]
+            send_ref[c * NS + s] = jnp.where(lane1 < NB, left, right)[:, : 2 * NB]
     for store in stores:
         store.wait()
 
@@ -193,7 +193,7 @@
     where = (lax.axis_index("outer") * NS + lax.axis_index(NEAR)).reshape(1).astype(jnp.int32)
     where, idx = lax.optimization_barrier((where, idx))
     send, res = pick(idx, g, r)
-    got = lax.all_to_all(send, NEAR + ("outer",), 0, 0)
+    got = lax.all_to_all(send, ("outer",) + NEAR, 0, 0)
     everyone = lax.all_to_all(copies(got), FAR, 0, 0)
     new = total(where, everyone, params.reshape(1024, 128))
     both = lax.all_to_all(new, ("outer",) + NEAR, 0, 0)

time: 58.2 us -> 58.1 us (level)
  no operation moved by 1% of the time
where the time goes in v6:
time: 58.1 us; the launch traced here: 57.5 us
  blocking collectives  51.4 us (88%)
  Pallas kernels  4.55 us (8%)
  local copies, waits for them, and re-layouts  0.83 us (1%)
  between operations  0.66 us (1%)
    all_to_all x1, blocking collectives, shards(): everyone = lax.all_to_all(copies(got), FAR, 0, 0)  23.9 us
    all_to_all x1, blocking collectives, shards(): got = lax.all_to_all(send, ('outer',) + NEAR, 0, 0)  14.7 us
    all_to_all x1, blocking collectives, shards(): both = lax.all_to_all(new, ('outer',) + NEAR, 0, 0)  12.8 us
    pallas_call x1, Pallas kernels, pick(): pl.pallas_call(pick_kernel, in_specs=[in_vmem, in_hbm, in_hbm], out_specs...  2.79 us
    pallas_call x1, Pallas kernels, total(): pl.pallas_call(total_kernel, grid_spec=pltpu.PrefetchScalarGridSpec(num_s...  1.67 us

profile of v6, /device:TPU:1, one launch (start us, length us, event | category | flops | bytes accessed | tf_op | source)
XLA Modules:
  0.0 57.5 jit_solution(4127577290212245374)
XLA Ops:
  0.6 2.8 %pick.1 = (f32[16,1,64]{2,1,0:T(1,128)S(1)}, f32[1024,128]{1,0:T(8,128)}) custom-call(s32[4,128]{1,0:T(4,128)} %bitcast.11, f32[1024,128]{1,0:T(8,128)} %bitcast.8, f32[1024,128]{1,0:T(8,128)} %bitcast.9), custom_call_target="tpu_custom_call" | custom-call | tf_op jit(solution)/shard_map/pick/pallas_call | solution.py:75
  3.4 14.7 %all_to_all.15.in_ref = f32[16,1,64]{2,1,0:T(1,128)S(1)} all-to-all(f32[16,1,64]{2,1,0:T(1,128)S(1)} %get-tuple-element.8), channel_id=1, replica_groups=mesh['x1'=2,'x0'=2,'y2'=2,'y1'=2,'y0'=2,'z2'=2,'z1'=2,'z0'=2,'outer'=2] ..., dimensions={0} | all-to-all | bytes 8192 | tf_op jit(solution)/shard_map/all_to_all | solution.py:196
  18.2 0.1 copies.1
  18.3 23.9 %all_to_all.16.w_ref = f32[32,8,128]{2,1,0:T(8,128)S(1)} all-to-all(f32[32,8,128]{2,1,0:T(8,128)S(1)} %copies.1), channel_id=1, replica_groups=mesh['x1'=2,'x0'=2,'y2'=2,'y1'=2,'y0'=2,'z2'=2,'z1'=2,'z0'=2,'outer'=2] ..., dimensions={0} | all-to-all | bytes 262144 | tf_op jit(solution)/shard_map/all_to_all | solution.py:197
  42.1 1.7 %total.1 = f32[16,64,128]{2,1,0:T(8,128)S(1)} custom-call(s32[1]{0:T(128)} %bitcast.where_ref, f32[32,8,128]{2,1,0:T(8,128)S(1)} %all_to_all.16.w_ref, f32[1024,128]{1,0:T(8,128)} %bitcast.10), custom_call_target="tpu_custom_call" | custom-call | tf_op jit(solution)/shard_map/total/pallas_call | solution.py:172
  43.8 12.8 %all_to_all.17 = f32[16,64,128]{2,1,0:T(8,128)S(1)} all-to-all(f32[16,64,128]{2,1,0:T(8,128)S(1)} %total.1), channel_id=1, replica_groups=mesh['x1'=2,'x0'=2,'y2'=2,'y1'=2,'y0'=2,'z2'=2,'z1'=2,'z0'=2,'outer'=2] ..., dimensions={0} | all-to-all | bytes 1048576 | tf_op jit(solution)/shard_map/all_to_all | solution.py:199
  56.6 0.8 %copy.7 = f32[131072]{0:T(1024)} copy(f32[131072]{0:T(1024)S(1)} %bitcast.7) | data formatting | bytes 1048576
